TPU v7x, 32 devices: a whole 2x2x4 slice. The times are simulated.
32 devices in a mesh: dp: 16 (over z, y, x), shard: 2 (over core).
Axes of the slice: x: 2, y: 2, z: 4, core: 2. Of those that a mesh axis runs over, the one named last changes fastest.
Arguments:
- features: bfloat16 [65536, 1024], P('dp'), may hold values from -150 to 150
- shared_weight: bfloat16 [1024, 2048], P(None, 'shard'), may hold values from -0.1875 to 0.1875
- task_heads: bfloat16 [6, 2048], P(None, 'shard'), may hold values from -0.4 to 0.4
- labels: int32 [65536, 6], P('dp'), may hold values from 0 to 1
- task_masks: int32 [65536, 6], P('dp'), may hold values from 0 to 1
- task_weights: float32 [6], replicated, may hold values from 0.5 to 2
- initial_losses: float32 [6], replicated, may hold values from 0.2 to 1
Outputs:
- update: float32 [1024, 2048], P('dp', 'shard')
- new_weights: float32 [6], replicated
All inputs are finite; a program needn't handle non-finite values.
Results may differ from a plain program's by a relative error of at most 0.00089.
Values sent between devices are 32-bit elements; how exact they have to be, the bound alone decides.
A program may use at most 256 MiB of HBM per device.

v0:
```python
import functools
import jax
import jax.numpy as jnp
from jax import lax
from jax.experimental import pallas as pl
from jax.experimental.pallas import tpu as pltpu
from jax.sharding import PartitionSpec as P

epsilon = 1e-06
learn_rate = 0.5
asymmetry = 1.5
MESH = pl.DeviceIdType.MESH
LAGS = (3, 6, 8, 10)


def silu_parts(preact):
    sigmoid_pre = jax.nn.sigmoid(preact)
    return (preact * sigmoid_pre, sigmoid_pre * (1.0 + preact * (1.0 - sigmoid_pre)))


def exchange_orders(task_count, levels):
    if levels == 4:
        table = ((0, 1, 2, 3), (1, 0, 2, 3), (2, 0, 1, 3), (0, 1, 2, 3), (1, 0, 2, 3), (2, 1, 0, 3))
        return [table[task % 6] for task in range(task_count)]
    return [tuple((task + level) % levels for level in range(levels)) for task in range(task_count)]


def stage_lags(levels):
    if levels == 4:
        return LAGS
    return tuple(3 + 2 * level for level in range(levels))


def partner_of(me, bit):
    mine = (me // (1 << bit)) % 2
    return me + (1 - 2 * mine) * (1 << bit)


def reduce_kernel(
    task_count,
    levels,
    shard_levels,
    entries,
    features,
    slope,
    errors,
    heads,
    stats,
    weights,
    initial,
    update,
    renewed,
    turned,
    rows_in,
    slope_in,
    terms,
    grads,
    *rest,
):
    landed = rest[:levels]
    mine_sum, their_sum, row_sem, slope_sem, send_sem, recv_sem, sum_send, sum_recv = rest[levels:]
    me = lax.axis_index("dp")
    my_shard = lax.axis_index("shard")
    samples, width_in = features.shape
    columns = terms.shape[1]
    blocks = slope.shape[1] // columns
    row_block = rows_in.shape[1]
    tile = min(256, width_in)
    tiles = width_in // tile
    tile_bits = tiles.bit_length() - 1
    orders = exchange_orders(task_count, levels)
    lags = stage_lags(levels)
    dp_partner = [partner_of(me, bit) for bit in range(levels)]
    shard_partner = [partner_of(my_shard, bit) for bit in range(shard_levels)]
    my_bit = [(me // (1 << bit)) % 2 for bit in range(levels)]

    barrier = pltpu.get_barrier_semaphore()
    for bit in range(levels):
        pl.semaphore_signal(
            barrier, inc=1, device_id=(dp_partner[bit], my_shard), device_id_type=MESH
        )
    for bit in range(shard_levels):
        pl.semaphore_signal(
            barrier, inc=1, device_id=(me, shard_partner[bit]), device_id_type=MESH
        )

    def load_rows(index):
        return pltpu.make_async_copy(
            features.at[pl.ds(index * row_block, row_block), :],
            rows_in.at[index % 2],
            row_sem.at[index % 2],
        )

    def load_slope(block, slot):
        return pltpu.make_async_copy(
            slope.at[:, pl.ds(pl.multiple_of(block * columns, columns), columns)],
            slope_in.at[slot],
            slope_sem.at[slot],
        )

    load_rows(0).start()
    for index in range(samples // row_block):
        if index + 1 < samples // row_block:
            load_rows(index + 1).start()
        load_rows(index).wait()
        turned[:, index * row_block : (index + 1) * row_block] = rows_in[index % 2].T
        if index == 0:
            load_slope(0, 0).start()
    pl.semaphore_wait(barrier, levels + shard_levels)

    def compute(block, slot, task):
        head = heads[task : task + 1, pl.ds(pl.multiple_of(block * columns, columns), columns)]

        def fill(step, carry):
            rows = pl.ds(pl.multiple_of(step * 256, 256), 256)
            scaled = errors[rows, task : task + 1] * slope_in[slot, rows, :]
            terms[rows, :] = (scaled * head).astype(jnp.bfloat16)
            return carry

        lax.fori_loop(0, samples // 256, fill, 0)

        def multiply(step, carry):
            rows = pl.ds(pl.multiple_of(step * tile, tile), tile)
            product = jnp.dot(turned[rows, :], terms[...], preferred_element_type=jnp.float32)
            high = tuple((step // (1 << bit)) % 2 for bit in range(tile_bits - 1, -1, -1))
            shape = grads.shape[1 + tile_bits :]
            grads[(task,) + high] = product.reshape(shape)
            return carry

        lax.fori_loop(0, tiles, multiply, 0)

    def part_of(block, task, stage, side):
        order = orders[task]
        left = [bit for bit in range(levels - 1, -1, -1) if bit not in order[:stage]]
        chosen = [side if bit == order[stage] else slice(None) for bit in left]
        if stage == 0:
            return grads, (task, *chosen)
        return landed[stage - 1], (block * task_count + task, *chosen)

    def exchange(block, task, stage):
        bit = orders[task][stage]
        chunk = block * task_count + task
        source, where = part_of(block, task, stage, 1 - my_bit[bit])
        return pltpu.make_async_remote_copy(
            src_ref=source.at[where],
            dst_ref=landed[stage].at[chunk],
            send_sem=send_sem.at[chunk, stage],
            recv_sem=recv_sem.at[chunk, stage],
            device_id=(dp_partner[bit], my_shard),
            device_id_type=MESH,
        )

    def combine(block, task, stage):
        bit = orders[task][stage]
        chunk = block * task_count + task
        exchange(block, task, stage).wait()
        source, where = part_of(block, task, stage, my_bit[bit])
        landed[stage][chunk] = landed[stage][chunk] + source[where]
        if stage + 1 < levels:
            exchange(block, task, stage + 1).start()

    def stages(block, task, guard):
        for stage in range(levels):
            earlier = task - lags[stage]
            of_task = earlier % task_count
            of_block = block + earlier // task_count
            if guard:

                @pl.when(of_block >= 0)
                def _():
                    combine(of_block, of_task, stage)
            else:
                if of_block < blocks and of_block >= 0:
                    combine(of_block, of_task, stage)

    def block_step(block, carry):
        slot = block % 2
        load_slope(block, slot).wait()

        @pl.when(block + 1 < blocks)
        def _():
            load_slope(block + 1, 1 - slot).start()

        for task in range(task_count):
            compute(block, slot, task)
            exchange(block, task, 0).start()
            stages(block, task, True)
        return carry

    lax.fori_loop(0, blocks, block_step, 0)
    for tick in range(lags[-1]):
        stages(blocks + tick // task_count, tick % task_count, False)

    final = landed[levels - 1]
    row = lax.broadcasted_iota(jnp.int32, (8, 128), 0)
    lane = lax.broadcasted_iota(jnp.int32, (8, 128), 1)
    total = stats[...]
    for one in range(task_count):
        for other in range(one, task_count):
            product = final[one] * final[other]
            for block in range(1, blocks):
                base = block * task_count
                product = product + final[base + one] * final[base + other]
            inner = jnp.sum(jnp.sum(product, axis=0, keepdims=True), axis=1, keepdims=True)
            here = ((row == one) & (lane == other)) | ((row == other) & (lane == one))
            total = jnp.where(here, inner, total)
    mine_sum[0] = total
    steps = [(me, partner) for partner in shard_partner]
    steps += [(partner, my_shard) for partner in dp_partner]
    for step, device in enumerate(steps):
        copy = pltpu.make_async_remote_copy(
            src_ref=mine_sum.at[step],
            dst_ref=their_sum.at[step],
            send_sem=sum_send.at[step],
            recv_sem=sum_recv.at[step],
            device_id=device,
            device_id_type=MESH,
        )
        copy.start()
        copy.wait()
        total = total + their_sum[step]
        if step + 1 < len(steps):
            mine_sum[step + 1] = total

    is_task = row[:, :1] < task_count
    diagonal = jnp.sum(jnp.where(row == lane, total, 0.0), axis=1, keepdims=True)
    losses = total[:, task_count : task_count + 1]

    def over_tasks(values):
        return jnp.sum(jnp.where(is_task, values, 0.0), axis=0, keepdims=True)

    root_mean = jnp.sqrt(diagonal / entries + epsilon)
    scaled = weights[...] * root_mean
    average = over_tasks(scaled) / task_count
    loss_ratio = losses / initial[...]
    relative = loss_ratio / (over_tasks(loss_ratio) / task_count)
    target = average * (relative * jnp.sqrt(relative))
    distance = (scaled - target) / average
    raised = weights[...] * jnp.exp(-learn_rate * distance)
    fresh = task_count * raised / over_tasks(raised)
    renewed[...] = jnp.broadcast_to(fresh, (8, 128))
    fresh = jnp.where(is_task, fresh, 0.0)
    across = jnp.sum(jnp.where(row == lane, fresh, 0.0), axis=0, keepdims=True)
    gram = jnp.where((row < task_count) & (lane < task_count), total, 0.0)
    inner = jnp.sum(gram * across, axis=1, keepdims=True)
    mean_square = jnp.sum(inner * fresh, axis=0, keepdims=True) / entries
    gain = lax.rsqrt(mean_square + epsilon)
    for block in range(blocks):
        base = block * task_count
        combined = fresh[0:1] * final[base]
        for task in range(1, task_count):
            combined = combined + fresh[task : task + 1] * final[base + task]
        update[:, block * columns : (block + 1) * columns] = combined * gain


def reduce_gradients(
    features, slope, errors, heads, stats, weights, initial, levels, shard_levels, entries
):
    samples, width_in = features.shape
    local_hidden = slope.shape[1]
    task_count = heads.shape[0]
    columns = min(256, local_hidden)
    chunks = (local_hidden // columns) * task_count
    rows = width_in >> levels
    row_block = min(512, samples)
    sums = levels + shard_levels
    vmem = pl.BlockSpec(memory_space=pltpu.VMEM)
    anywhere = pl.BlockSpec(memory_space=pl.ANY)
    landed = [
        pltpu.VMEM((chunks,) + (2,) * (levels - 1 - stage) + (rows, columns), jnp.float32)
        for stage in range(levels)
    ]
    return pl.pallas_call(
        functools.partial(reduce_kernel, task_count, levels, shard_levels, entries),
        out_shape=(
            jax.ShapeDtypeStruct((rows, local_hidden), jnp.float32),
            jax.ShapeDtypeStruct((8, 128), jnp.float32),
        ),
        in_specs=[anywhere, anywhere, vmem, vmem, vmem, vmem, vmem],
        out_specs=(vmem, vmem),
        scratch_shapes=[
            pltpu.VMEM((width_in, samples), jnp.bfloat16),
            pltpu.VMEM((2, row_block, width_in), jnp.bfloat16),
            pltpu.VMEM((2, samples, columns), jnp.float32),
            pltpu.VMEM((samples, columns), jnp.bfloat16),
            pltpu.VMEM((task_count,) + (2,) * levels + (rows, columns), jnp.float32),
            *landed,
            pltpu.VMEM((sums, 8, 128), jnp.float32),
            pltpu.VMEM((sums, 8, 128), jnp.float32),
            pltpu.SemaphoreType.DMA((2,)),
            pltpu.SemaphoreType.DMA((2,)),
            pltpu.SemaphoreType.DMA((chunks, levels)),
            pltpu.SemaphoreType.DMA((chunks, levels)),
            pltpu.SemaphoreType.DMA((sums,)),
            pltpu.SemaphoreType.DMA((sums,)),
        ],
        compiler_params=pltpu.CompilerParams(
            collective_id=0, has_side_effects=True, vmem_limit_bytes=62 * 1024 * 1024
        ),
        name="reduce_gradients",
    )(features, slope, errors, heads, stats, weights, initial)


def sum_over_shard(partial, shard_count):
    if shard_count == 2:
        return partial + lax.ppermute(partial, "shard", [(0, 1), (1, 0)])
    return lax.psum(partial, "shard")


def on_device(
    features, shared_weight, task_heads, labels, task_masks, task_weights, initial_losses
):
    shard_count = lax.axis_size("shard")
    replica_count = lax.axis_size("dp")
    width_in = features.shape[1]
    local_hidden = shared_weight.shape[1]
    task_count = task_heads.shape[0]
    entries = width_in * local_hidden * shard_count
    total_samples = features.shape[0] * replica_count
    levels = replica_count.bit_length() - 1
    shard_levels = shard_count.bit_length() - 1
    preact = jnp.dot(features, shared_weight, preferred_element_type=jnp.float32)
    activated, silu_slope = silu_parts(preact)
    hidden = activated.astype(jnp.bfloat16)
    partial_logits = lax.dot_general(
        task_heads, hidden, (((1,), (1,)), ((), ())), preferred_element_type=jnp.float32
    )
    logits = sum_over_shard(partial_logits, shard_count)
    targets = labels.T.astype(jnp.float32)
    mask_float = task_masks.T.astype(jnp.float32)
    loss_part = (
        jnp.sum(mask_float * (jax.nn.softplus(logits) - targets * logits), axis=1) / total_samples
    )
    errors = (mask_float * (jax.nn.sigmoid(logits) - targets)).T
    lane = lax.broadcasted_iota(jnp.int32, (8, 128), 1)
    padding = 8 - task_count
    loss_column = jnp.pad(loss_part / shard_count, (0, padding))[:, None]
    stats = jnp.where(lane == task_count, loss_column, 0.0)
    update, renewed = reduce_gradients(
        features,
        silu_slope,
        errors,
        task_heads.astype(jnp.float32),
        stats,
        jnp.pad(task_weights, (0, padding), constant_values=1.0)[:, None],
        jnp.pad(initial_losses, (0, padding), constant_values=1.0)[:, None],
        levels,
        shard_levels,
        entries,
    )
    return (update, renewed[:task_count, 0])


def solution(mesh):
    return jax.shard_map(
        on_device,
        mesh=mesh,
        in_specs=(
            P("dp", None),
            P(None, "shard"),
            P(None, "shard"),
            P("dp", None),
            P("dp", None),
            P(),
            P(),
        ),
        out_specs=(P("dp", "shard"), P()),
        check_vma=False,
    )
```

profile of v0, /device:TPU:0, one launch (start us, length us, event | category | flops | bytes accessed | tf_op | source)
XLA Modules:
  0.0 269.9 jit_solution(10287535372104415439)
XLA Ops:
  0.6 0.0 copy-start.2
  0.6 22.0 %add_multiply_fusion = (f32[4096,1024]{1,0:T(8,128)}, f32[4096,1024]{1,0:T(8,128)}) fusion(bf16[4096,1024]{1,0:T(8,128)(2,1)} %features.1, bf16[1024,1024]{1,0:T(8,128)(2,1)} %param.8), kind=kOutput, calls=%fused_computation.1 | convolution fusion | flops 8619294720 | bytes 44040192 | tf_op jit(solution)/shard_map/dot_general | solution.py:322
  22.6 0.0 copy-done.2
  22.6 8.3 %fusion.1 = f32[6,4096]{0,1:T(8,128)S(1)} fusion(bf16[6,1024]{1,0:T(8,128)(2,1)S(1)} %copy-done.2, f32[4096,1024]{1,0:T(8,128)} %get-tuple-element.9), kind=kOutput, calls=%fused_computation.5 | convolution fusion | flops 71303168 | bytes 16887808 | tf_op jit(solution)/shard_map/dot_general | solution.py:325
  30.9 0.0 copy-start
  30.9 0.0 copy-start.1
  30.9 0.6 copy.28
  31.5 0.5 collective-permute-start
  32.1 0.6 convert_element_type.25.heads
  32.7 0.0 copy-done
  32.7 0.0 copy-start.3
  32.7 0.0 copy-start.4
  32.7 2.0 copy.26
  34.7 0.0 copy-done.1
  34.7 1.9 copy.32
  36.7 0.0 copy-done.3
  36.7 0.7 copy.33.weights
  37.3 0.0 copy-done.4
  37.3 0.7 copy.34.initial
  38.0 0.0 collective-permute-done
  38.0 1.9 copy.29
  40.0 6.1 %fusion.4 = (f32[6]{0:T(128)S(1)}, f32[4096,6]{1,0:T(8,128)}) fusion(f32[4096,6]{1,0:T(8,128)} %copy.32, f32[4096,6]{1,0:T(8,128)} %copy.26, f32[6,4096]{0,1:T(8,128)S(1)} %fusion.1, f32[6,4096]{0,1:T(8,128)} %copy.29), kind=kLoop, calls=%fused_computation.8 | loop fusion | flops 393210 | bytes 491544 | tf_op jit(solution)/shard_map/reduce_sum | solution.py:332
  46.0 0.7 broadcast_select_fusion.stats
  46.7 220.2 %reduce_gradients.1 = (f32[64,1024]{1,0:T(8,128)}, f32[8,128]{1,0:T(8,128)}) custom-call(bf16[4096,1024]{1,0:T(8,128)(2,1)} %features.1, f32[4096,1024]{1,0:T(8,128)} %get-tuple-element.8.slope, f32[4096,6]{1,0:T(8,128)} %get-tuple-element.7.errors, f32[6,1024]{1,0:T(8,128)} %convert_element_type.25.heads, f32[8,128]{1,0:T(8,128)} %broadcast_select_fusion.stats, ...), custom_call_target="tpu_custom_call" | custom-call | tf_op jit(solution)/shard_map/reduce_gradients/pallas_call | solution.py:273
  267.0 1.3 slice_reduce_fusion
  268.3 1.7 copy.39
  (7 shorter events, 0.0 us)
Async XLA Ops:
  0.6 22.0 %copy-start.2 = (bf16[6,1024]{1,0:T(8,128)(2,1)S(1)}, bf16[6,1024]{1,0:T(8,128)(2,1)}, u32[]{:S(2)}) copy-start(bf16[6,1024]{1,0:T(8,128)(2,1)} %param.9) | copy-start | bytes 36868
  30.9 1.8 copy-start
  30.9 3.8 %copy-start.1 = (s32[4096,6]{0,1:T(8,128)S(1)}, s32[4096,6]{0,1:T(8,128)}, u32[]{:S(2)}) copy-start(s32[4096,6]{0,1:T(8,128)} %param.10) | copy-start | bytes 294916
  31.5 6.5 %collective-permute-start = (f32[6,4096]{1,0:T(8,128)S(1)}, f32[6,4096]{1,0:T(8,128)S(1)}, u32[]{:S(2)}, u32[]{:S(2)}) collective-permute-start(f32[6,4096]{1,0:T(8,128)S(1)} %copy.28), channel_id=1, source_target_pairs={{0,1},{1,0},{2,3},{3,2},{4,5},{5,4},{6,7},{7,6},{8,9},{9,8},{10,11... | collective-permute-start | bytes 294920 | tf_op jit(solution)/shard_map/ppermute | solution.py:306
  32.7 4.0 %copy-start.3 = (f32[6]{0:T(128)S(1)}, f32[6]{0:T(128)}, u32[]{:S(2)}) copy-start(f32[6]{0:T(128)} %param.12) | copy-start | bytes 76
  32.7 4.6 %copy-start.4 = (f32[6]{0:T(128)S(1)}, f32[6]{0:T(128)}, u32[]{:S(2)}) copy-start(f32[6]{0:T(128)} %param.13) | copy-start | bytes 76
where the time goes:
time: 270 us
  Pallas kernels  220 us (81%)
  matrix products  30.2 us (11%)
  local copies, waits for them, and re-layouts  10.8 us (4%)
  other arithmetic  7.37 us (3%)
    pallas_call x1, Pallas kernels, reduce_gradients(): pl.pallas_call(functools.partial(reduce_kernel, task_count, levels, shard...  220 us
    dot_general x1, matrix products, on_device(): jnp.dot(features, shared_weight, preferred_element_type=jnp.float32)  22 us
    dot_general x1, matrix products, on_device(): lax.dot_general(task_heads, hidden, (((1,), (1,)), ((), ())), preferred_e...  8.27 us
    reduce_sum x1, other arithmetic, on_device(): jnp.sum(mask_float * (jax.nn.softplus(logits) - targets * logits), axis=1)  6.06 us
  transfers between devices with their start and end apart: 1, of which 0 were waited for; matrix products, arithmetic and copies ran while one was open for 2% of the time, Pallas kernels for 0%

commit v1 on v0

v1 whole, which is shorter than its diff:
```python
import functools
import jax
import jax.numpy as jnp
from jax import lax
from jax.experimental import pallas as pl
from jax.experimental.pallas import tpu as pltpu
from jax.sharding import PartitionSpec as P

epsilon = 1e-06
learn_rate = 0.5
asymmetry = 1.5
MESH = pl.DeviceIdType.MESH
LAGS = (4, 8, 12, 16)
ROW_BLOCK = 512
FILL_ROWS = 1024


def silu_parts(preact):
    sigmoid_pre = jax.nn.sigmoid(preact)
    return (preact * sigmoid_pre, sigmoid_pre * (1.0 + preact * (1.0 - sigmoid_pre)))


def exchange_orders(count, levels):
    if levels == 4:
        table = ((0, 1, 2, 3), (1, 0, 2, 3), (2, 0, 1, 3), (0, 1, 2, 3), (1, 0, 2, 3), (2, 1, 0, 3))
        return [table[index % 6] for index in range(count)]
    return [tuple((index + level) % levels for level in range(levels)) for index in range(count)]


def stage_lags(levels):
    if levels == 4:
        return LAGS
    return tuple(4 + 4 * level for level in range(levels))


def partner_of(me, bit):
    mine = (me // (1 << bit)) % 2
    return me + (1 - 2 * mine) * (1 << bit)


def reduce_kernel(
    task_count,
    levels,
    shard_levels,
    entries,
    total_samples,
    features,
    shared,
    heads,
    labels,
    masks,
    weights,
    initial,
    update,
    renewed,
    turned,
    rows_in,
    slope,
    errors,
    logits,
    other_logits,
    terms,
    grads,
    *rest,
):
    landed = rest[:levels]
    pair_sum, other_sum, all_sums, row_sem, send_sem, recv_sem = rest[levels : levels + 6]
    logit_send, logit_recv, pair_send, pair_recv, share_send, share_recv = rest[levels + 6 :]
    me = lax.axis_index("dp")
    my_shard = lax.axis_index("shard")
    replicas = 1 << levels
    samples, width_in = features.shape
    local_hidden = shared.shape[1]
    columns = terms.shape[1]
    blocks = local_hidden // columns
    row_block = rows_in.shape[1]
    row_blocks = samples // row_block
    lanes = grads.shape[-1]
    halves = columns // lanes
    pieces = task_count * halves
    slots = grads.shape[0]
    tile = min(512, width_in)
    tiles = width_in // tile
    tile_bits = tiles.bit_length() - 1
    orders = exchange_orders(pieces, levels)
    lags = stage_lags(levels)
    dp_partner = [partner_of(me, bit) for bit in range(levels)]
    shard_partner = [partner_of(my_shard, bit) for bit in range(shard_levels)]
    my_bit = [(me // (1 << bit)) % 2 for bit in range(levels)]

    barrier = pltpu.get_barrier_semaphore()
    for offset in range(1, replicas):
        pl.semaphore_signal(
            barrier, inc=1, device_id=((me + offset) % replicas, my_shard), device_id_type=MESH
        )
    for bit in range(shard_levels):
        pl.semaphore_signal(
            barrier, inc=1, device_id=(me, shard_partner[bit]), device_id_type=MESH
        )

    def load_rows(index):
        return pltpu.make_async_copy(
            features.at[pl.ds(pl.multiple_of(index * row_block, row_block), row_block), :],
            rows_in.at[index % 2],
            row_sem.at[index % 2],
        )

    load_rows(0).start()

    def front(index, carry):
        @pl.when(index + 1 < row_blocks)
        def _():
            load_rows(index + 1).start()

        load_rows(index).wait()
        inputs = rows_in[index % 2]
        rows = pl.ds(pl.multiple_of(index * row_block, row_block), row_block)
        turned[:, rows] = inputs.T
        partial = jnp.zeros((row_block, task_count), jnp.float32)
        for block in range(blocks):
            part = slice(block * columns, (block + 1) * columns)
            preact = jnp.dot(inputs, shared[:, part], preferred_element_type=jnp.float32)
            activated, silu_slope = silu_parts(preact)
            slope[rows, part] = silu_slope
            partial = partial + lax.dot_general(
                activated.astype(jnp.bfloat16),
                heads[:, part],
                (((1,), (1,)), ((), ())),
                preferred_element_type=jnp.float32,
            )
        logits[0, :, rows] = partial.T
        return carry

    lax.fori_loop(0, row_blocks, front, 0)
    pl.semaphore_wait(barrier, replicas - 1 + shard_levels)
    for level in range(shard_levels):
        copy = pltpu.make_async_remote_copy(
            src_ref=logits.at[level],
            dst_ref=other_logits.at[level],
            send_sem=logit_send.at[level],
            recv_sem=logit_recv.at[level],
            device_id=(me, shard_partner[level]),
            device_id_type=MESH,
        )
        copy.start()
        copy.wait()
        logits[level + 1] = logits[level] + other_logits[level]
    whole = logits[shard_levels]
    targets = labels[...].astype(jnp.float32)
    mask_float = masks[...].astype(jnp.float32)
    loss = jnp.sum(
        mask_float * (jax.nn.softplus(whole) - targets * whole), axis=1, keepdims=True
    ) / (total_samples * (1 << shard_levels))
    flat_errors = mask_float * (jax.nn.sigmoid(whole) - targets)
    errors[...] = flat_errors.T

    fill_rows = min(FILL_ROWS, samples)

    def compute(block, task):
        part = pl.ds(pl.multiple_of(block * columns, columns), columns)
        head = heads[task : task + 1, part].astype(jnp.float32)

        def fill(step, carry):
            rows = pl.ds(pl.multiple_of(step * fill_rows, fill_rows), fill_rows)
            scaled = errors[rows, task : task + 1] * slope[rows, part]
            terms[rows, :] = (scaled * head).astype(jnp.bfloat16)
            return carry

        lax.fori_loop(0, samples // fill_rows, fill, 0)

        def multiply(step, carry):
            rows = pl.ds(pl.multiple_of(step * tile, tile), tile)
            product = jnp.dot(turned[rows, :], terms[...], preferred_element_type=jnp.float32)
            high = tuple((step // (1 << bit)) % 2 for bit in range(tile_bits - 1, -1, -1))
            shape = grads.shape[2 + tile_bits :]
            for half in range(halves):
                part = product[:, half * lanes : (half + 1) * lanes]
                grads[(task % slots, half) + high] = part.reshape(shape)
            return carry

        lax.fori_loop(0, tiles, multiply, 0)

    def part_of(block, piece, stage, side):
        order = orders[piece]
        left = [bit for bit in range(levels - 1, -1, -1) if bit not in order[:stage]]
        chosen = [side if bit == order[stage] else slice(None) for bit in left]
        if stage == 0:
            return grads, ((piece // halves) % slots, piece % halves, *chosen)
        return landed[stage - 1], (block * pieces + piece, *chosen)

    def exchange(block, piece, stage):
        bit = orders[piece][stage]
        index = block * pieces + piece
        source, where = part_of(block, piece, stage, 1 - my_bit[bit])
        return pltpu.make_async_remote_copy(
            src_ref=source.at[where],
            dst_ref=landed[stage].at[index],
            send_sem=send_sem.at[index, stage],
            recv_sem=recv_sem.at[index, stage],
            device_id=(dp_partner[bit], my_shard),
            device_id_type=MESH,
        )

    def combine(block, piece, stage):
        bit = orders[piece][stage]
        index = block * pieces + piece
        exchange(block, piece, stage).wait()
        source, where = part_of(block, piece, stage, my_bit[bit])
        landed[stage][index] = landed[stage][index] + source[where]
        if stage + 1 < levels:
            exchange(block, piece, stage + 1).start()

    def stages(block, piece, guard):
        for stage in range(levels):
            earlier = piece - lags[stage]
            of_piece = earlier % pieces
            of_block = block + earlier // pieces
            if guard:

                @pl.when(of_block >= 0)
                def _():
                    combine(of_block, of_piece, stage)
            else:
                if of_block < blocks and of_block >= 0:
                    combine(of_block, of_piece, stage)

    def block_step(block, carry):
        for task in range(task_count):
            compute(block, task)
            for piece in range(task * halves, (task + 1) * halves):
                exchange(block, piece, 0).start()
            for piece in range(task * halves, (task + 1) * halves):
                stages(block, piece, True)
        return carry

    lax.fori_loop(0, blocks, block_step, 0)
    for tick in range(lags[-1]):
        stages(blocks + tick // pieces, tick % pieces, False)

    final = landed[levels - 1]
    row = lax.broadcasted_iota(jnp.int32, (8, 128), 0)
    lane = lax.broadcasted_iota(jnp.int32, (8, 128), 1)
    total = jnp.zeros((8, 128), jnp.float32)
    for task in range(task_count):
        here = (row == task) & (lane == task_count)
        total = jnp.where(here, loss[task : task + 1], total)
    for one in range(task_count):
        for other in range(one, task_count):
            product = 0.0
            for block in range(blocks):
                for half in range(halves):
                    base = block * pieces + half
                    product = product + final[base + one * halves] * final[base + other * halves]
            inner = jnp.sum(jnp.sum(product, axis=0, keepdims=True), axis=1, keepdims=True)
            here = ((row == one) & (lane == other)) | ((row == other) & (lane == one))
            total = jnp.where(here, inner, total)
    for level in range(shard_levels):
        pair_sum[level] = total
        copy = pltpu.make_async_remote_copy(
            src_ref=pair_sum.at[level],
            dst_ref=other_sum.at[level],
            send_sem=pair_send.at[level],
            recv_sem=pair_recv.at[level],
            device_id=(me, shard_partner[level]),
            device_id_type=MESH,
        )
        copy.start()
        copy.wait()
        total = total + other_sum[level]
    all_sums[me] = total

    def share(offset, owner):
        return pltpu.make_async_remote_copy(
            src_ref=all_sums.at[me],
            dst_ref=all_sums.at[owner],
            send_sem=share_send.at[offset - 1],
            recv_sem=share_recv.at[owner],
            device_id=((me + offset) % replicas, my_shard),
            device_id_type=MESH,
        )

    for offset in range(1, replicas):
        share(offset, me).start()
    for offset in range(1, replicas):
        share(offset, (me + offset) % replicas).wait_recv()
    for offset in range(1, replicas):
        share(offset, me).wait_send()
    total = all_sums[0]
    for device in range(1, replicas):
        total = total + all_sums[device]

    is_task = row[:, :1] < task_count
    diagonal = jnp.sum(jnp.where(row == lane, total, 0.0), axis=1, keepdims=True)
    losses = total[:, task_count : task_count + 1]

    def over_tasks(values):
        return jnp.sum(jnp.where(is_task, values, 0.0), axis=0, keepdims=True)

    def column_of(values):
        column = jnp.ones((8, 1), jnp.float32)
        for task in range(task_count):
            column = jnp.where(row[:, :1] == task, values[task], column)
        return column

    start_weights = column_of(weights)
    root_mean = jnp.sqrt(diagonal / entries + epsilon)
    scaled = start_weights * root_mean
    average = over_tasks(scaled) / task_count
    loss_ratio = losses / column_of(initial)
    relative = loss_ratio / (over_tasks(loss_ratio) / task_count)
    target = average * (relative * jnp.sqrt(relative))
    distance = (scaled - target) / average
    raised = start_weights * jnp.exp(-learn_rate * distance)
    fresh = task_count * raised / over_tasks(raised)
    fresh = jnp.where(is_task, fresh, 0.0)
    across = jnp.sum(jnp.where(row == lane, fresh, 0.0), axis=0, keepdims=True)
    renewed[...] = across[:, :task_count]
    gram = jnp.where((row < task_count) & (lane < task_count), total, 0.0)
    inner = jnp.sum(gram * across, axis=1, keepdims=True)
    mean_square = jnp.sum(inner * fresh, axis=0, keepdims=True) / entries
    gain = lax.rsqrt(mean_square + epsilon)
    for block in range(blocks):
        for half in range(halves):
            base = block * pieces + half
            combined = fresh[0:1] * final[base]
            for task in range(1, task_count):
                combined = combined + fresh[task : task + 1] * final[base + task * halves]
            start = block * columns + half * lanes
            update[:, start : start + lanes] = combined * gain


def reduce_gradients(
    features, shared, heads, labels, masks, weights, initial, replica_count, shard_count
):
    samples, width_in = features.shape
    local_hidden = shared.shape[1]
    task_count = heads.shape[0]
    levels = replica_count.bit_length() - 1
    shard_levels = shard_count.bit_length() - 1
    entries = width_in * local_hidden * shard_count
    columns = min(256, local_hidden)
    lanes = min(128, columns)
    halves = columns // lanes
    chunks = (local_hidden // columns) * task_count * halves
    slots = 3 if task_count % 3 == 0 else task_count
    pairs = max(shard_levels, 1)
    rows = width_in // replica_count
    row_block = min(ROW_BLOCK, samples)
    vmem = pl.BlockSpec(memory_space=pltpu.VMEM)
    smem = pl.BlockSpec(memory_space=pltpu.SMEM)
    anywhere = pl.BlockSpec(memory_space=pl.ANY)
    landed = [
        pltpu.VMEM((chunks,) + (2,) * (levels - 1 - stage) + (rows, lanes), jnp.float32)
        for stage in range(levels)
    ]
    return pl.pallas_call(
        functools.partial(
            reduce_kernel,
            task_count,
            levels,
            shard_levels,
            entries,
            samples * replica_count,
        ),
        out_shape=(
            jax.ShapeDtypeStruct((rows, local_hidden), jnp.float32),
            jax.ShapeDtypeStruct((1, task_count), jnp.float32),
        ),
        in_specs=[anywhere, vmem, vmem, vmem, vmem, smem, smem],
        out_specs=(vmem, vmem),
        scratch_shapes=[
            pltpu.VMEM((width_in, samples), jnp.bfloat16),
            pltpu.VMEM((2, row_block, width_in), jnp.bfloat16),
            pltpu.VMEM((samples, local_hidden), jnp.float32),
            pltpu.VMEM((samples, task_count), jnp.float32),
            pltpu.VMEM((shard_levels + 1, task_count, samples), jnp.float32),
            pltpu.VMEM((pairs, task_count, samples), jnp.float32),
            pltpu.VMEM((samples, columns), jnp.bfloat16),
            pltpu.VMEM((slots, halves) + (2,) * levels + (rows, lanes), jnp.float32),
            *landed,
            pltpu.VMEM((pairs, 8, 128), jnp.float32),
            pltpu.VMEM((pairs, 8, 128), jnp.float32),
            pltpu.VMEM((replica_count, 8, 128), jnp.float32),
            pltpu.SemaphoreType.DMA((2,)),
            pltpu.SemaphoreType.DMA((chunks, levels)),
            pltpu.SemaphoreType.DMA((chunks, levels)),
            pltpu.SemaphoreType.DMA((pairs,)),
            pltpu.SemaphoreType.DMA((pairs,)),
            pltpu.SemaphoreType.DMA((pairs,)),
            pltpu.SemaphoreType.DMA((pairs,)),
            pltpu.SemaphoreType.DMA((replica_count - 1,)),
            pltpu.SemaphoreType.DMA((replica_count,)),
        ],
        compiler_params=pltpu.CompilerParams(
            collective_id=0, has_side_effects=True, vmem_limit_bytes=67043328
        ),
        name="reduce_gradients",
    )(features, shared, heads, labels, masks, weights, initial)


def on_device(
    features, shared_weight, task_heads, labels, task_masks, task_weights, initial_losses
):
    update, renewed = reduce_gradients(
        features,
        shared_weight,
        task_heads,
        labels.T,
        task_masks.T,
        task_weights,
        initial_losses,
        lax.axis_size("dp"),
        lax.axis_size("shard"),
    )
    return (update, renewed[0])


def solution(mesh):
    return jax.shard_map(
        on_device,
        mesh=mesh,
        in_specs=(
            P("dp", None),
            P(None, "shard"),
            P(None, "shard"),
            P("dp", None),
            P("dp", None),
            P(),
            P(),
        ),
        out_specs=(P("dp", "shard"), P()),
        check_vma=False,
    )
```

time: 270 us -> 225 us (0.83)
  matrix products: 30.2 us -> 0 us
  local copies, waits for them, and re-layouts: 10.8 us -> 2.8 us
  other arithmetic: 7.37 us -> 0 us
    dot_general x2 -> x0, matrix products: 30.2 us -> none  [the longest x1 22 us: on_device(): jnp.dot(features, shared_weight, preferred_element_type=jnp.float32)]
    reduce_sum x1 -> x0, other arithmetic: 6.06 us -> none  [on_device(): jnp.sum(mask_float * (jax.nn.softplus(logits) - targets * logits), axis=1)]
    convert_element_type x2 -> x0, local copies, waits for them, and re-layouts: 3.92 us -> none  [the longest x1 1.97 us: on_device(): mask_float = task_masks.T.astype(jnp.float32)]
  transfers between devices with their start and end apart: 1 -> 0, of which waited for: 0 -> 0; matrix products, arithmetic and copies ran while one was open for 2% -> 0% of each run, Pallas kernels for 0% -> 0%
where the time goes in v1:
time: 225 us
  Pallas kernels  222 us (99%)
  local copies, waits for them, and re-layouts  2.8 us (1%)
    pallas_call x1, Pallas kernels, reduce_gradients(): pl.pallas_call(functools.partial(reduce_kernel, task_count, levels, shard...  222 us

profile of v1, /device:TPU:0, one launch (start us, length us, event | category | flops | bytes accessed | tf_op | source)
XLA Modules:
  0.0 225.2 jit_solution(13043079716647537059)
XLA Ops:
  0.6 221.8 %reduce_gradients.1 = (f32[64,1024]{1,0:T(8,128)}, f32[1,6]{1,0:T(1,128)}) custom-call(bf16[4096,1024]{1,0:T(8,128)(2,1)} %features.1, bf16[1024,1024]{1,0:T(8,128)(2,1)} %shared.1, bf16[6,1024]{1,0:T(8,128)(2,1)} %heads.1, s32[6,4096]{1,0:T(8,128)} %bitcast.3, s32[6,4096]{1,0:T(8,128)} %bitcast.4, f32[6]{0:T(128)} %weights.1, f32[6]{0:T(128)} %initial.1), custom_call_target="tpu_custom_call" | custom-call | tf_op jit(solution)/shard_map/reduce_gradients/pallas_call | solution.py:356
  222.4 1.7 copy.11
  224.1 1.1 copy.12

commit v2 on v1

--- a/solution.py
+++ b/solution.py
@@ -10,7 +10,7 @@
 learn_rate = 0.5
 asymmetry = 1.5
 MESH = pl.DeviceIdType.MESH
-LAGS = (4, 8, 12, 16)
+LAGS = (4, 4, 8, 8, 12, 12, 16)
 ROW_BLOCK = 512
 FILL_ROWS = 1024
 
@@ -30,7 +30,7 @@
 def stage_lags(levels):
     if levels == 4:
         return LAGS
-    return tuple(4 + 4 * level for level in range(levels))
+    return tuple(4 + 4 * (step // 2) for step in range(2 * levels - 1))
 
 
 def partner_of(me, bit):
@@ -45,7 +45,7 @@
     entries,
     total_samples,
     features,
-    shared,
+    shared_hbm,
     heads,
     labels,
     masks,
@@ -55,23 +55,28 @@
     renewed,
     turned,
     rows_in,
+    shared,
     slope,
     errors,
     logits,
     other_logits,
-    terms,
+    even_terms,
+    odd_terms,
     grads,
     *rest,
 ):
     landed = rest[:levels]
-    pair_sum, other_sum, all_sums, row_sem, send_sem, recv_sem = rest[levels : levels + 6]
-    logit_send, logit_recv, pair_send, pair_recv, share_send, share_recv = rest[levels + 6 :]
+    pair_sum, other_sum, all_sums = rest[levels : levels + 3]
+    row_sem, weight_sem, send_sem, recv_sem = rest[levels + 3 : levels + 7]
+    logit_send, logit_recv, pair_send, pair_recv, share_send, share_recv = rest[levels + 7 :]
     me = lax.axis_index("dp")
     my_shard = lax.axis_index("shard")
     replicas = 1 << levels
+    terms = (even_terms, odd_terms)
+    hidden = odd_terms
     samples, width_in = features.shape
     local_hidden = shared.shape[1]
-    columns = terms.shape[1]
+    columns = even_terms.shape[1]
     blocks = local_hidden // columns
     row_block = rows_in.shape[1]
     row_blocks = samples // row_block
@@ -105,7 +110,22 @@
             row_sem.at[index % 2],
         )
 
+    load_weight = pltpu.make_async_copy(shared_hbm, shared, weight_sem.at[0])
+    load_weight.start()
     load_rows(0).start()
+    load_weight.wait()
+
+    def store_logits(index):
+        partial = jnp.zeros((row_block, task_count), jnp.float32)
+        for block in range(blocks):
+            partial = partial + lax.dot_general(
+                hidden[block * row_block : (block + 1) * row_block, :],
+                heads[:, block * columns : (block + 1) * columns],
+                (((1,), (1,)), ((), ())),
+                preferred_element_type=jnp.float32,
+            )
+        rows = pl.ds(pl.multiple_of(index * row_block, row_block), row_block)
+        logits[0, :, rows] = partial.T
 
     def front(index, carry):
         @pl.when(index + 1 < row_blocks)
@@ -116,22 +136,18 @@
         inputs = rows_in[index % 2]
         rows = pl.ds(pl.multiple_of(index * row_block, row_block), row_block)
         turned[:, rows] = inputs.T
-        partial = jnp.zeros((row_block, task_count), jnp.float32)
+        store_logits(jnp.maximum(index - 1, 0))
         for block in range(blocks):
             part = slice(block * columns, (block + 1) * columns)
             preact = jnp.dot(inputs, shared[:, part], preferred_element_type=jnp.float32)
             activated, silu_slope = silu_parts(preact)
             slope[rows, part] = silu_slope
-            partial = partial + lax.dot_general(
-                activated.astype(jnp.bfloat16),
-                heads[:, part],
-                (((1,), (1,)), ((), ())),
-                preferred_element_type=jnp.float32,
-            )
-        logits[0, :, rows] = partial.T
+            hidden[block * row_block : (block + 1) * row_block, :] = activated.astype(jnp.bfloat16)
         return carry
 
+    hidden[...] = jnp.zeros_like(hidden)
     lax.fori_loop(0, row_blocks, front, 0)
+    store_logits(row_blocks - 1)
     pl.semaphore_wait(barrier, replicas - 1 + shard_levels)
     for level in range(shard_levels):
         copy = pltpu.make_async_remote_copy(
@@ -154,23 +170,28 @@
     flat_errors = mask_float * (jax.nn.sigmoid(whole) - targets)
     errors[...] = flat_errors.T
 
-    fill_rows = min(FILL_ROWS, samples)
+    def fill(block, task, start, count):
+        part = pl.ds(pl.multiple_of(block * columns, columns), columns)
+        rows = pl.ds(pl.multiple_of(start, count), count)
+        scaled = errors[rows, task : task + 1] * slope[rows, part]
+        head = heads[task : task + 1, part].astype(jnp.float32)
+        terms[task % 2][rows, :] = (scaled * head).astype(jnp.bfloat16)
+
+    def fill_first(step, carry):
+        fill(0, 0, step * FILL_ROWS, FILL_ROWS)
+        return carry
 
     def compute(block, task):
-        part = pl.ds(pl.multiple_of(block * columns, columns), columns)
-        head = heads[task : task + 1, part].astype(jnp.float32)
-
-        def fill(step, carry):
-            rows = pl.ds(pl.multiple_of(step * fill_rows, fill_rows), fill_rows)
-            scaled = errors[rows, task : task + 1] * slope[rows, part]
-            terms[rows, :] = (scaled * head).astype(jnp.bfloat16)
-            return carry
-
-        lax.fori_loop(0, samples // fill_rows, fill, 0)
+        following = (task + 1) % task_count
+        next_block = jnp.minimum(block + (task + 1) // task_count, blocks - 1)
+        share_rows = samples // tiles
 
         def multiply(step, carry):
             rows = pl.ds(pl.multiple_of(step * tile, tile), tile)
-            product = jnp.dot(turned[rows, :], terms[...], preferred_element_type=jnp.float32)
+            product = jnp.dot(
+                turned[rows, :], terms[task % 2][...], preferred_element_type=jnp.float32
+            )
+            fill(next_block, following, step * share_rows, share_rows)
             high = tuple((step // (1 << bit)) % 2 for bit in range(tile_bits - 1, -1, -1))
             shape = grads.shape[2 + tile_bits :]
             for half in range(halves):
@@ -207,22 +228,26 @@
         exchange(block, piece, stage).wait()
         source, where = part_of(block, piece, stage, my_bit[bit])
         landed[stage][index] = landed[stage][index] + source[where]
-        if stage + 1 < levels:
-            exchange(block, piece, stage + 1).start()
+
+    def advance(block, piece, step):
+        if step % 2 == 0:
+            combine(block, piece, step // 2)
+        else:
+            exchange(block, piece, (step + 1) // 2).start()
 
     def stages(block, piece, guard):
-        for stage in range(levels):
-            earlier = piece - lags[stage]
+        for step, lag in enumerate(lags):
+            earlier = piece - lag
             of_piece = earlier % pieces
             of_block = block + earlier // pieces
             if guard:
 
                 @pl.when(of_block >= 0)
                 def _():
-                    combine(of_block, of_piece, stage)
+                    advance(of_block, of_piece, step)
             else:
                 if of_block < blocks and of_block >= 0:
-                    combine(of_block, of_piece, stage)
+                    advance(of_block, of_piece, step)
 
     def block_step(block, carry):
         for task in range(task_count):
@@ -233,6 +258,7 @@
                 stages(block, piece, True)
         return carry
 
+    lax.fori_loop(0, samples // FILL_ROWS, fill_first, 0)
     lax.fori_loop(0, blocks, block_step, 0)
     for tick in range(lags[-1]):
         stages(blocks + tick // pieces, tick % pieces, False)
@@ -366,15 +392,17 @@
             jax.ShapeDtypeStruct((rows, local_hidden), jnp.float32),
             jax.ShapeDtypeStruct((1, task_count), jnp.float32),
         ),
-        in_specs=[anywhere, vmem, vmem, vmem, vmem, smem, smem],
+        in_specs=[anywhere, anywhere, vmem, vmem, vmem, smem, smem],
         out_specs=(vmem, vmem),
         scratch_shapes=[
             pltpu.VMEM((width_in, samples), jnp.bfloat16),
             pltpu.VMEM((2, row_block, width_in), jnp.bfloat16),
+            pltpu.VMEM((width_in, local_hidden), jnp.bfloat16),
             pltpu.VMEM((samples, local_hidden), jnp.float32),
             pltpu.VMEM((samples, task_count), jnp.float32),
             pltpu.VMEM((shard_levels + 1, task_count, samples), jnp.float32),
             pltpu.VMEM((pairs, task_count, samples), jnp.float32),
+            pltpu.VMEM((samples, columns), jnp.bfloat16),
             pltpu.VMEM((samples, columns), jnp.bfloat16),
             pltpu.VMEM((slots, halves) + (2,) * levels + (rows, lanes), jnp.float32),
             *landed,
@@ -382,6 +410,7 @@
             pltpu.VMEM((pairs, 8, 128), jnp.float32),
             pltpu.VMEM((replica_count, 8, 128), jnp.float32),
             pltpu.SemaphoreType.DMA((2,)),
+            pltpu.SemaphoreType.DMA((1,)),
             pltpu.SemaphoreType.DMA((chunks, levels)),
             pltpu.SemaphoreType.DMA((chunks, levels)),
             pltpu.SemaphoreType.DMA((pairs,)),

time: 225 us -> 220 us (0.978)
  Pallas kernels: 222 us -> 217 us
    pallas_call x1, Pallas kernels: 222 us -> 217 us  [reduce_gradients(): pl.pallas_call(functools.partial(reduce_kernel, task_count, levels, shard...]
where the time goes in v2:
time: 220 us
  Pallas kernels  217 us (99%)
  local copies, waits for them, and re-layouts  2.8 us (1%)
    pallas_call x1, Pallas kernels, reduce_gradients(): pl.pallas_call(functools.partial(reduce_kernel, task_count, levels, shard...  217 us

profile of v2, /device:TPU:0, one launch (start us, length us, event | category | flops | bytes accessed | tf_op | source)
XLA Modules:
  0.0 220.2 jit_solution(13288460084458383254)
XLA Ops:
  0.6 216.8 %reduce_gradients.1 = (f32[64,1024]{1,0:T(8,128)}, f32[1,6]{1,0:T(1,128)}) custom-call(bf16[4096,1024]{1,0:T(8,128)(2,1)} %features.1, bf16[1024,1024]{1,0:T(8,128)(2,1)} %shared_hbm.1, bf16[6,1024]{1,0:T(8,128)(2,1)} %heads.1, s32[6,4096]{1,0:T(8,128)} %bitcast.3, s32[6,4096]{1,0:T(8,128)} %bitcast.4, f32[6]{0:T(128)} %weights.1, f32[6]{0:T(128)} %initial.1), custom_call_target="tpu_custom_call" | custom-call | tf_op jit(solution)/shard_map/reduce_gradients/pallas_call | solution.py:382
  217.4 1.7 copy.11
  219.1 1.1 copy.12

commit v3 on v2

--- a/solution.py
+++ b/solution.py
@@ -116,14 +116,15 @@
     load_weight.wait()
 
     def store_logits(index):
-        partial = jnp.zeros((row_block, task_count), jnp.float32)
-        for block in range(blocks):
-            partial = partial + lax.dot_general(
-                hidden[block * row_block : (block + 1) * row_block, :],
-                heads[:, block * columns : (block + 1) * columns],
-                (((1,), (1,)), ((), ())),
-                preferred_element_type=jnp.float32,
-            )
+        parts = [
+            hidden[block * row_block : (block + 1) * row_block, :] for block in range(blocks)
+        ]
+        partial = lax.dot_general(
+            jnp.concatenate(parts, axis=1),
+            heads[...],
+            (((1,), (1,)), ((), ())),
+            preferred_element_type=jnp.float32,
+        )
         rows = pl.ds(pl.multiple_of(index * row_block, row_block), row_block)
         logits[0, :, rows] = partial.T
 

time: 220 us -> 220 us (level)
  no operation moved by 1% of the time
where the time goes in v3:
time: 220 us
  Pallas kernels  217 us (99%)
  local copies, waits for them, and re-layouts  2.8 us (1%)
    pallas_call x1, Pallas kernels, reduce_gradients(): pl.pallas_call(functools.partial(reduce_kernel, task_count, levels, shard...  217 us

profile of v3, /device:TPU:0, one launch (start us, length us, event | category | flops | bytes accessed | tf_op | source)
XLA Modules:
  0.0 220.2 jit_solution(2987334163414531940)
XLA Ops:
  0.6 216.8 %reduce_gradients.1 = (f32[64,1024]{1,0:T(8,128)}, f32[1,6]{1,0:T(1,128)}) custom-call(bf16[4096,1024]{1,0:T(8,128)(2,1)} %features.1, bf16[1024,1024]{1,0:T(8,128)(2,1)} %shared_hbm.1, bf16[6,1024]{1,0:T(8,128)(2,1)} %heads.1, s32[6,4096]{1,0:T(8,128)} %bitcast.3, s32[6,4096]{1,0:T(8,128)} %bitcast.4, f32[6]{0:T(128)} %weights.1, f32[6]{0:T(128)} %initial.1), custom_call_target="tpu_custom_call" | custom-call | tf_op jit(solution)/shard_map/reduce_gradients/pallas_call | solution.py:383
  217.4 1.7 copy.11
  219.1 1.1 copy.12
